TPU v7x, 32 devices: a whole 2x2x4 slice. The times are simulated.
32 devices in a mesh: rep: 16 (over z, y, core), tp: 2 (over x).
Axes of the slice: x: 2, y: 2, z: 4, core: 2. Of those that a mesh axis runs over, the one named last changes fastest.
Arguments:
- activations: bfloat16 [8192, 6144], P('rep', 'tp'), may hold values from -6 to 6
- norm_gain: float32 [6144], replicated, may hold values from 0.5 to 1.5
- query_gain: float32 [128], replicated, may hold values from 0.5 to 18
- key_gain: float32 [128], replicated, may hold values from 0.5 to 18
- project_in: bfloat16 [6144, 24, 384], P('rep', 'tp'), may hold values from -1 to 1
- project_out: bfloat16 [6144, 3072], P('rep', 'tp'), may hold values from -1 to 1
Outputs:
- attended: bfloat16 [8192, 6144], P('rep', 'tp')
- weight_norms: float32 [2], replicated
All inputs are finite; a program needn't handle non-finite values.
Results may differ from a plain program's by a relative error of at most 0.018.
The roundings to bfloat16 on the way count: a program that leaves them out, or rounds other values in their place, can miss the bound.
Values may be sent and summed in bfloat16 or wider, within the bound.
A program may use at most 192 MiB of HBM per device.

v0:
```python
import math
import jax
import jax.numpy as jnp
from jax import lax
from jax.sharding import PartitionSpec as P

D = 6144
HEADS = 24
HEAD_DIM = 128
PATCHES = 256


def layer_norm(values, gain):
    average = jnp.mean(values, -1, keepdims=True)
    centred = values - average
    variance = jnp.mean(centred * centred, -1, keepdims=True)
    return centred * lax.rsqrt(variance + 1e-06) * gain


def shards(activations, norm_gain, query_gain, key_gain, project_in, project_out):
    gathered_rows = lax.all_gather(activations, "tp", axis=1, tiled=True)
    normed = layer_norm(gathered_rows.astype(jnp.float32), norm_gain).astype(jnp.bfloat16)
    tok_rows = normed.shape[0]
    local_heads = project_in.shape[1]
    head_dim = project_in.shape[2] // 3
    piece = lax.all_gather(project_in, "rep", axis=0, tiled=True)
    running = jnp.dot(normed, piece.reshape(piece.shape[0], -1), preferred_element_type=jnp.float32)
    projected = running
    images_here = tok_rows // PATCHES
    projected = projected.reshape(images_here, PATCHES, local_heads, 3 * head_dim)
    queries = layer_norm(projected[..., :head_dim], query_gain).astype(jnp.bfloat16)
    keys_normed = layer_norm(projected[..., head_dim : 2 * head_dim], key_gain).astype(jnp.bfloat16)
    values = projected[..., 2 * head_dim :].astype(jnp.bfloat16)
    scores = jnp.einsum(
        "iphd,iqhd->ihpq", queries, keys_normed, preferred_element_type=jnp.float32
    ) / math.sqrt(head_dim)
    probabilities = jax.nn.softmax(scores, axis=-1).astype(jnp.bfloat16)
    mixed = jnp.einsum("ihpq,iqhd->iphd", probabilities, values, preferred_element_type=jnp.float32)
    mixed = mixed.astype(jnp.bfloat16).reshape(tok_rows, local_heads * head_dim)
    product = lax.dot_general(
        mixed,
        lax.all_gather(project_out, "rep", axis=0, tiled=True),
        (((1,), (1,)), ((), ())),
        preferred_element_type=jnp.float32,
    )
    attended = lax.psum_scatter(product.astype(jnp.bfloat16), "tp", scatter_dimension=1, tiled=True)
    local_in = jnp.sum(jnp.square(project_in.astype(jnp.float32)))
    local_out = jnp.sum(jnp.square(project_out.astype(jnp.float32)))
    total_in, total_out = lax.psum((local_in, local_out), ("rep", "tp"))
    weight_norms = jnp.stack([jnp.sqrt(total_in / (3 * HEADS * HEAD_DIM)), jnp.sqrt(total_out / D)])
    return (attended, weight_norms)


def solution(mesh):
    in_specs = (P("rep", "tp"), P(), P(), P(), P("rep", "tp", None), P("rep", "tp"))
    out_specs = (P("rep", "tp"), P())
    return jax.shard_map(shards, mesh=mesh, in_specs=in_specs, out_specs=out_specs, check_vma=False)
```

profile of v0, /device:TPU:0, one launch (start us, length us, event | category | flops | bytes accessed | tf_op | source)
XLA Modules:
  0.0 571.8 jit_solution(6341764529476445264)
XLA Ops:
  7.2 0.0 all-gather.4.cloned.1.call-start
  7.2 0.7 all-gather.4.cloned.1.call-update
  7.9 0.0 all-gather.6.cloned.1.call-start
  7.9 6.0 %copy.10 = bf16[384,12,384]{0,2,1:T(8,128)(2,1)} copy(bf16[384,12,384]{2,0,1:T(8,128)(2,1)} %param.10) | data formatting | bytes 7077888 | tf_op args[4]
  14.0 0.0 all-gather.6.cloned.1.call-update
  14.0 0.0 all-gather.8.cloned.1.call-start
  14.1 0.0 copy-start.3
  14.1 0.7 all-gather.8.cloned.1.call-update
  14.7 0.0 reduce-scatter.2.cloned.1.call-start
  14.8 77.8 %all-gather.4.cloned.1.call-done = bf16[512,6144]{1,0:T(8,128)(2,1)} async-done(((bf16[512,3072]{1,0:T(8,128)(2,1)}), bf16[512,6144]{1,0:T(8,128)(2,1)}) %all-gather.4.cloned.1.call-update) | async-done | bytes 6291472 | tf_op jit(solution)/shard_map/all_gather | solution.py:21
  92.6 0.0 copy-start
  92.6 3.8 convert_reduce_fusion
  96.5 0.7 copy-done
  97.2 1.8 fusion.5
  99.0 0.0 copy-done.3
  99.0 6.3 %fusion.7 = bf16[512,6144]{1,0:T(8,128)(2,1)} fusion(bf16[512,6144]{1,0:T(8,128)(2,1)S(1)} %copy-done, f32[6144]{0:T(1024)S(1)} %copy-done.3, f32[512]{0:T(512)S(1)} %add_rsqrt_fusion.2, f32[512]{0:T(512)S(1)} %broadcast_multiply_fusion.2), kind=kLoop, calls=%fused_computation.9 | loop fusion | flops 15728640 | bytes 12611584 | tf_op jit(solution)/shard_map/convert_element_type | solution.py:22
  105.3 265.2 %all-gather.6.cloned.1.call-done = bf16[6144,12,384]{0,2,1:T(8,128)(2,1)} async-done(((bf16[384,12,384]{0,2,1:T(8,128)(2,1)}), bf16[6144,12,384]{0,2,1:T(8,128)(2,1)}) %all-gather.6.cloned.1.call-update) | async-done | bytes 56623120 | tf_op jit(solution)/shard_map/all_gather | solution.py:26
  370.5 37.1 %fusion.1 = f32[2,256,12,384]{3,1,2,0:T(8,128)} fusion(bf16[2,256,6144,1]{2,1,3,0:T(8,128)(2,1)} %bitcast.26, bf16[6144,12,384]{0,2,1:T(8,128)(2,1)} %all-gather.6.cloned.1.call-done), kind=kOutput, calls=%fused_computation.1 | convolution fusion | flops 28991029248 | bytes 72351744 | tf_op jit(solution)/shard_map/dot_general | solution.py:27
  407.6 0.0 copy-start.1
  407.6 0.0 copy-start.4
  407.6 0.0 copy-start.5
  407.6 4.7 slice_reduce_fusion.1
  412.4 5.8 %multiply_reduce_fusion.3 = (f32[2,256,12]{1,2,0:T(8,128)S(1)}, f32[2,256,12]{1,2,0:T(8,128)S(1)}) fusion(f32[2,256,12,384]{3,1,2,0:T(8,128)} %fusion.1, f32[2,256,12]{1,2,0:T(8,128)S(1)} %get-tuple-element.11, f32[2,256,12]{1,2,0:T(8,128)S(1)} %get-tuple-element.10), kind=kLoop, calls=%fused_computation.21 | loop fusion | flops 4706304 | bytes 6389760 | tf_op jit(solution)/shard_map/reduce_sum | solution.py:16
  418.3 0.0 copy-done.1
  418.3 0.0 copy-done.4
  418.3 0.0 copy-done.5
  418.3 3.5 fusion.14
  421.8 5.0 fusion.23
  426.8 0.9 fusion.21
  427.7 1.6 copy.13
  429.3 0.3 copy.17
  429.7 41.3 %all-gather.8.cloned.1.call-done = bf16[6144,1536]{1,0:T(8,128)(2,1)} async-done(((bf16[384,1536]{1,0:T(8,128)(2,1)}), bf16[6144,1536]{1,0:T(8,128)(2,1)}) %all-gather.8.cloned.1.call-update) | async-done | bytes 18874384 | tf_op jit(solution)/shard_map/all_gather | solution.py:42
  471.0 15.6 %convolution_convert_fusion = bf16[512,6144]{1,0:T(8,128)(2,1)} fusion(bf16[512,1536]{0,1:T(8,128)(2,1)S(1)} %bitcast.28, bf16[6144,1536]{1,0:T(8,128)(2,1)} %all-gather.8.cloned.1.call-done), kind=kOutput, calls=%fused_computation.10 | convolution fusion | flops 9666822144 | bytes 26738688 | tf_op jit(solution)/shard_map/dot_general | solution.py:40
  486.6 0.0 copy-start.2
  486.6 0.0 reduce-scatter.2.cloned.1.call-update
  486.6 2.0 copy-done.2
  488.6 2.4 multiply_reduce_fusion
  491.0 2.5 multiply_reduce_fusion.4
  493.5 41.4 %all-reduce = (f32[]{:T(128)}, f32[]{:T(128)}) all-reduce(f32[]{:T(128)} %multiply_reduce_fusion.4, f32[]{:T(128)} %multiply_reduce_fusion), channel_id=1, replica_groups=mesh['rep'=16,'tp'=2] {'rep','tp'}, use_global_device_ids=true, to_apply=%region_12.0 | all-reduce | flops 2 | bytes 16 | tf_op jit(solution)/shard_map/psum | solution.py:49
  536.2 0.6 pad_maximum_fusion
  536.8 28.5 %reduce-scatter.2.cloned.1.call-done = bf16[512,3072]{1,0:T(8,128)(2,1)} async-done(((bf16[512,6144]{1,0:T(8,128)(2,1)}), bf16[512,3072]{1,0:T(8,128)(2,1)}) %reduce-scatter.2.cloned.1.call-update) | async-done | bytes 3145744 | tf_op jit(solution)/shard_map/reduce_scatter | solution.py:46
  (5 shorter events, 0.0 us)
Async XLA Ops:
  7.2 85.5 %all-gather.4.cloned.1.call-start = ((), (), s32[]{:S(2)}) async-start(), calls=%async_computation.1 | async-start | bytes 9437184 | tf_op jit(solution)/shard_map/all_gather | solution.py:21
  7.9 362.6 %all-gather.6.cloned.1.call-start = ((), (), s32[]{:S(2)}) async-start(), calls=%async_computation.2 | async-start | bytes 60162048 | tf_op jit(solution)/shard_map/all_gather | solution.py:26
  14.0 457.0 %all-gather.8.cloned.1.call-start = ((), (), s32[]{:S(2)}) async-start(), calls=%async_computation.3 | async-start | bytes 20054016 | tf_op jit(solution)/shard_map/all_gather | solution.py:42
  14.1 85.0 %copy-start.3 = (f32[6144]{0:T(1024)S(1)}, f32[6144]{0:T(1024)}, u32[]{:S(2)}) copy-start(f32[6144]{0:T(1024)} %param.7) | copy-start | bytes 73732
  14.7 550.6 %reduce-scatter.2.cloned.1.call-start = ((), (), s32[]{:S(2)}) async-start(), calls=%async_computation.4 | async-start | bytes 9437184 | tf_op jit(solution)/shard_map/reduce_scatter | solution.py:46
  92.6 4.6 copy-start
  407.6 10.6 %copy-start.1 = (f32[2,256,12,384]{3,1,2,0:T(8,128)S(1)}, f32[2,256,12,384]{3,1,2,0:T(8,128)}, u32[]{:S(2)}) copy-start(f32[2,256,12,384]{3,1,2,0:T(8,128)} %fusion.1) | copy-start | bytes 28311556
  407.6 10.6 %copy-start.4 = (f32[128]{0:T(128)S(1)}, f32[128]{0:T(128)}, u32[]{:S(2)}) copy-start(f32[128]{0:T(128)} %param.9) | copy-start | bytes 1540
  407.6 10.6 %copy-start.5 = (f32[128]{0:T(128)S(1)}, f32[128]{0:T(128)}, u32[]{:S(2)}) copy-start(f32[128]{0:T(128)} %param.8) | copy-start | bytes 1540
  486.6 2.0 copy-start.2
Sparse Core Ops, SparseCore 0:
  9.5 83.0 all-gather.3
  94.2 276.2 all-gather.5
  372.1 98.8 all-gather.7
  486.8 78.5 reduce-scatter.1
where the time goes:
time: 572 us
  waiting for transfers between devices  414 us (72%)
  matrix products  57.2 us (10%)
  blocking collectives  41.4 us (7%)
  other arithmetic  33 us (6%)
  between operations  15.2 us (3%)
  local copies, waits for them, and re-layouts  10.7 us (2%)
    all_gather x1, waiting for transfers between devices, shards(): piece = lax.all_gather(project_in, 'rep', axis=0, tiled=True)  265 us
    all_gather x1, waiting for transfers between devices, shards(): gathered_rows = lax.all_gather(activations, 'tp', axis=1, tiled=True)  77.8 us
    psum x1, blocking collectives, shards(): total_in, total_out = lax.psum((local_in, local_out), ('rep', 'tp'))  41.4 us
    all_gather x1, waiting for transfers between devices, shards(): lax.all_gather(project_out, 'rep', axis=0, tiled=True)  41.3 us
    dot_general x1, matrix products, shards(): jnp.dot(normed, piece.reshape(piece.shape[0], -1), preferred_element_type...  37.1 us
    reduce_scatter x1, waiting for transfers between devices, shards(): lax.psum_scatter(product.astype(jnp.bfloat16), 'tp', scatter_dimension=1,...  28.5 us
    dot_general x1, matrix products, shards(): lax.dot_general(mixed, lax.all_gather(project_out, 'rep', axis=0, tiled=T...  15.6 us
  transfers between devices with their start and end apart: 4, of which 4 were waited for; matrix products, arithmetic and copies ran while one was open for 14% of the time, Pallas kernels for 0%

commit v1 on v0

--- a/solution.py
+++ b/solution.py
@@ -8,6 +8,27 @@
 HEADS = 24
 HEAD_DIM = 128
 PATCHES = 256
+
+
+def ring_gather(value, axis, dim):
+    peers, here, extent = (lax.axis_size(axis), lax.axis_index(axis), value.shape[dim])
+    right = [(i, (i + 1) % peers) for i in range(peers)]
+    behind = [(i, (i - 1) % peers) for i in range(peers)]
+    out = jnp.zeros((*value.shape[:dim], peers * extent, *value.shape[dim + 1 :]), value.dtype)
+    out = lax.dynamic_update_slice_in_dim(out, value, here * extent, axis=dim)
+    from_left = from_right = value
+    half = peers // 2
+    for step in range(1, half + 1):
+        from_left = lax.ppermute(from_left, axis, right)
+        out = lax.dynamic_update_slice_in_dim(
+            out, from_left, (here - step) % peers * extent, axis=dim
+        )
+        if step < peers - half:
+            from_right = lax.ppermute(from_right, axis, behind)
+            out = lax.dynamic_update_slice_in_dim(
+                out, from_right, (here + step) % peers * extent, axis=dim
+            )
+    return out
 
 
 def layer_norm(values, gain):
@@ -23,7 +44,7 @@
     tok_rows = normed.shape[0]
     local_heads = project_in.shape[1]
     head_dim = project_in.shape[2] // 3
-    piece = lax.all_gather(project_in, "rep", axis=0, tiled=True)
+    piece = ring_gather(project_in, "rep", 0)
     running = jnp.dot(normed, piece.reshape(piece.shape[0], -1), preferred_element_type=jnp.float32)
     projected = running
     images_here = tok_rows // PATCHES

time: 572 us -> 860 us (1.50)
  starting transfers between devices: 0.16 us -> 526 us
  waiting for transfers between devices: 414 us -> 106 us
  local copies, waits for them, and re-layouts: 10.7 us -> 80 us
    ppermute x0 -> x15, starting transfers between devices: none -> 526 us  [the longest x8 517 us: ring_gather(): from_left = lax.ppermute(from_left, axis, right)]
    all_gather x1 -> x0, waiting for transfers between devices: 265 us -> none  [shards(): piece = lax.all_gather(project_in, 'rep', axis=0, tiled=True)]
    all_gather x1, waiting for transfers between devices: 77.8 us -> 0.01 us  [shards(): gathered_rows = lax.all_gather(activations, 'tp', axis=1, tiled=True)]
    ppermute x0 -> x15, waiting for transfers between devices: none -> 75.1 us  [the longest x8 75.1 us: ring_gather(): from_left = lax.ppermute(from_left, axis, right)]
    dynamic_update_slice x0 -> x16, local copies, waits for them, and re-layouts: none -> 51 us  [the longest x8 26.6 us: ring_gather(): lax.dynamic_update_slice_in_dim(out, from_left, (here - step) % peers * e...]
    all_gather x1, waiting for transfers between devices: 41.3 us -> 0.02 us  [shards(): lax.all_gather(project_out, 'rep', axis=0, tiled=True)]
    broadcast_in_dim x0 -> x1, local copies, waits for them, and re-layouts: none -> 17.9 us  [ring_gather(): jnp.zeros((*value.shape[:dim], peers * extent, *value.shape[dim + 1:]), v...]
  transfers between devices with their start and end apart: 4 -> 18, of which waited for: 4 -> 8; matrix products, arithmetic and copies ran while one was open for 14% -> 17% of each run, Pallas kernels for 0% -> 0%
where the time goes in v1:
time: 860 us; the launch traced here: 859 us
  starting transfers between devices  526 us (61%)
  waiting for transfers between devices  106 us (12%)
  local copies, waits for them, and re-layouts  80 us (9%)
  matrix products  57.2 us (7%)
  blocking collectives  42.4 us (5%)
  other arithmetic  32.9 us (4%)
  between operations  15.3 us (2%)
    ppermute x8, starting transfers between devices, ring_gather(): from_left = lax.ppermute(from_left, axis, right)  517 us
    ppermute x8, waiting for transfers between devices, ring_gather(): from_left = lax.ppermute(from_left, axis, right)  75.1 us
    psum x1, blocking collectives, shards(): total_in, total_out = lax.psum((local_in, local_out), ('rep', 'tp'))  42.4 us
    dot_general x1, matrix products, shards(): jnp.dot(normed, piece.reshape(piece.shape[0], -1), preferred_element_type...  37.1 us
    reduce_scatter x1, waiting for transfers between devices, shards(): lax.psum_scatter(product.astype(jnp.bfloat16), 'tp', scatter_dimension=1,...  29.9 us
    dynamic_update_slice x8, local copies, waits for them, and re-layouts, ring_gather(): lax.dynamic_update_slice_in_dim(out, from_left, (here - step) % peers * e...  26.6 us
    dynamic_update_slice x7, local copies, waits for them, and re-layouts, ring_gather(): lax.dynamic_update_slice_in_dim(out, from_right, (here + step) % peers *...  22.1 us
    broadcast_in_dim x1, local copies, waits for them, and re-layouts, ring_gather(): jnp.zeros((*value.shape[:dim], peers * extent, *value.shape[dim + 1:]), v...  17.9 us
  transfers between devices with their start and end apart: 18, of which 8 were waited for; matrix products, arithmetic and copies ran while one was open for 17% of the time, Pallas kernels for 0%

profile of v1, /device:TPU:0, one launch (start us, length us, event | category | flops | bytes accessed | tf_op | source)
XLA Modules:
  0.0 859.4 jit_solution(12576278534395171416)
XLA Ops:
  7.9 4.6 copy.10
  13.0 5.0 collective-permute-start.1
  18.1 39.3 %collective-permute-done = bf16[384,12,384]{0,2,1:T(8,128)(2,1)} collective-permute-done((bf16[384,12,384]{0,2,1:T(8,128)(2,1)S(1)}, bf16[384,12,384]{0,2,1:T(8,128)(2,1)}, u32[]{:S(2)}, u32[]{:S(2)}) %collective-permute-start) | collective-permute-done | bytes 3538976 | tf_op jit(solution)/shard_map/ppermute | solution.py:22
  57.4 34.6 %collective-permute-start.2 = (bf16[384,12,384]{0,2,1:T(8,128)(2,1)}, bf16[384,12,384]{0,2,1:T(8,128)(2,1)}, u32[]{:S(2)}, u32[]{:S(2)}) collective-permute-start(bf16[384,12,384]{0,2,1:T(8,128)(2,1)} %collective-permute-done), channel_id=1, source_target_pairs={{0,2},{2,4},{4,6},{6,8},{8,10},{10,12},{12,14},{14,16},{16,18},{18... | collective-permute-start | bytes 10616840 | tf_op jit(solution)/shard_map/ppermute | solution.py:22
  92.2 9.3 %collective-permute-done.2 = bf16[384,12,384]{0,2,1:T(8,128)(2,1)} collective-permute-done((bf16[384,12,384]{0,2,1:T(8,128)(2,1)}, bf16[384,12,384]{0,2,1:T(8,128)(2,1)}, u32[]{:S(2)}, u32[]{:S(2)}) %collective-permute-start.2) | collective-permute-done | bytes 3538976 | tf_op jit(solution)/shard_map/ppermute | solution.py:22
  101.4 182.7 %collective-permute-start.4 = (bf16[384,12,384]{0,2,1:T(8,128)(2,1)}, bf16[384,12,384]{0,2,1:T(8,128)(2,1)S(1)}, u32[]{:S(2)}, u32[]{:S(2)}) collective-permute-start(bf16[384,12,384]{0,2,1:T(8,128)(2,1)} %collective-permute-done.2), channel_id=1, source_target_pairs={{0,2},{2,4},{4,6},{6,8},{8,10},{10,12},{12,14},{14,16},{16,18},{18... | collective-permute-start | bytes 10616840 | tf_op jit(solution)/shard_map/ppermute | solution.py:22
  285.8 4.7 collective-permute-done.4
  290.6 82.2 %collective-permute-start.6 = (bf16[384,12,384]{0,2,1:T(8,128)(2,1)S(1)}, bf16[384,12,384]{0,2,1:T(8,128)(2,1)S(1)}, u32[]{:S(2)}, u32[]{:S(2)}) collective-permute-start(bf16[384,12,384]{0,2,1:T(8,128)(2,1)S(1)} %collective-permute-done.4), channel_id=1, source_target_pairs={{0,2},{2,4},{4,6},{6,8},{8,10},{10,12},{12,14},{14,16},{16,18},{18... | collective-permute-start | bytes 10616840 | tf_op jit(solution)/shard_map/ppermute | solution.py:22
  372.8 5.8 collective-permute-done.6
  378.6 72.9 %collective-permute-start.8 = (bf16[384,12,384]{0,2,1:T(8,128)(2,1)S(1)}, bf16[384,12,384]{0,2,1:T(8,128)(2,1)S(1)}, u32[]{:S(2)}, u32[]{:S(2)}) collective-permute-start(bf16[384,12,384]{0,2,1:T(8,128)(2,1)S(1)} %collective-permute-done.6), channel_id=1, source_target_pairs={{0,2},{2,4},{4,6},{6,8},{8,10},{10,12},{12,14},{14,16},{16,18},{18... | collective-permute-start | bytes 10616840 | tf_op jit(solution)/shard_map/ppermute | solution.py:22
  451.6 5.8 collective-permute-done.8
  457.3 73.0 %collective-permute-start.10 = (bf16[384,12,384]{0,2,1:T(8,128)(2,1)S(1)}, bf16[384,12,384]{0,2,1:T(8,128)(2,1)}, u32[]{:S(2)}, u32[]{:S(2)}) collective-permute-start(bf16[384,12,384]{0,2,1:T(8,128)(2,1)S(1)} %collective-permute-done.8), channel_id=1, source_target_pairs={{0,2},{2,4},{4,6},{6,8},{8,10},{10,12},{12,14},{14,16},{16,18},{18... | collective-permute-start | bytes 10616840 | tf_op jit(solution)/shard_map/ppermute | solution.py:22
  530.3 6.0 collective-permute-done.10
  536.3 34.9 %collective-permute-start.12 = (bf16[384,12,384]{0,2,1:T(8,128)(2,1)}, bf16[384,12,384]{0,2,1:T(8,128)(2,1)}, u32[]{:S(2)}, u32[]{:S(2)}) collective-permute-start(bf16[384,12,384]{0,2,1:T(8,128)(2,1)} %collective-permute-done.10), channel_id=1, source_target_pairs={{0,2},{2,4},{4,6},{6,8},{8,10},{10,12},{12,14},{14,16},{16,18},{18... | collective-permute-start | bytes 10616840 | tf_op jit(solution)/shard_map/ppermute | solution.py:22
  571.2 17.9 %broadcast_in_dim.2 = bf16[6144,12,384]{0,2,1:T(8,128)(2,1)} broadcast(bf16[]{:T(256)} %constant.112.clone.1), dimensions={} | broadcast | bytes 56623104 | tf_op jit(solution)/shard_map/broadcast_in_dim | solution.py:17
  589.1 2.3 constant_dynamic-update-slice_fusion.15
  591.5 4.3 constant_dynamic-update-slice_fusion.14
  595.7 4.3 constant_dynamic-update-slice_fusion.13
  600.0 3.8 convert_reduce_fusion
  604.6 1.8 fusion.5
  606.4 3.8 collective-permute-start.13
  610.2 4.3 collective-permute-done.12
  614.4 36.0 %collective-permute-start.14 = (bf16[384,12,384]{0,2,1:T(8,128)(2,1)}, bf16[384,12,384]{0,2,1:T(8,128)(2,1)S(1)}, u32[]{:S(2)}, u32[]{:S(2)}) collective-permute-start(bf16[384,12,384]{0,2,1:T(8,128)(2,1)} %collective-permute-done.12), channel_id=1, source_target_pairs={{0,2},{2,4},{4,6},{6,8},{8,10},{10,12},{12,14},{14,16},{16,18},{18... | collective-permute-start | bytes 10616840 | tf_op jit(solution)/shard_map/ppermute | solution.py:22
  650.5 6.2 fusion.7
  656.7 4.5 constant_dynamic-update-slice_fusion.12
  661.3 2.2 constant_dynamic-update-slice_fusion.11
  663.5 2.2 constant_dynamic-update-slice_fusion.10
  665.7 2.3 constant_dynamic-update-slice_fusion.9
  668.0 2.2 constant_dynamic-update-slice_fusion.8
  670.2 2.3 constant_dynamic-update-slice_fusion.7
  672.5 2.2 constant_dynamic-update-slice_fusion.6
  674.7 4.4 constant_dynamic-update-slice_fusion.5
  679.0 4.5 constant_dynamic-update-slice_fusion.4
  683.5 4.4 constant_dynamic-update-slice_fusion.3
  687.8 4.4 constant_dynamic-update-slice_fusion.2
  692.2 2.4 constant_dynamic-update-slice_fusion.1
  694.6 2.3 constant_dynamic-update-slice_fusion
  696.9 37.1 %fusion.1 = f32[2,256,12,384]{3,1,2,0:T(8,128)} fusion(bf16[2,256,6144,1]{2,1,3,0:T(8,128)(2,1)} %bitcast.26, bf16[6144,12,384]{0,2,1:T(8,128)(2,1)} %constant_dynamic-update-slice_fusion), kind=kOutput, calls=%fused_computation.1 | convolution fusion | flops 28991029248 | bytes 72351744 | tf_op jit(solution)/shard_map/dot_general | solution.py:48
  734.1 4.7 slice_reduce_fusion.1
  738.8 5.7 multiply_reduce_fusion.3
  744.5 3.5 fusion.14
  748.1 5.0 fusion.23
  756.0 15.6 %convolution_convert_fusion = bf16[512,6144]{1,0:T(8,128)(2,1)} fusion(bf16[512,1536]{0,1:T(8,128)(2,1)S(1)} %bitcast.28, bf16[6144,1536]{1,0:T(8,128)(2,1)} %all-gather.5.cloned.1.call-done), kind=kOutput, calls=%fused_computation.10 | convolution fusion | flops 9666822144 | bytes 26738688 | tf_op jit(solution)/shard_map/dot_general | solution.py:61
  771.7 2.0 copy-done.2
  773.6 2.5 multiply_reduce_fusion
  776.1 2.5 multiply_reduce_fusion.4
  778.6 42.4 %all-reduce = (f32[]{:T(128)}, f32[]{:T(128)}) all-reduce(f32[]{:T(128)} %multiply_reduce_fusion.4, f32[]{:T(128)} %multiply_reduce_fusion), channel_id=1, replica_groups=mesh['rep'=16,'tp'=2] {'rep','tp'}, use_global_device_ids=true, to_apply=%region_12.13 | all-reduce | flops 2 | bytes 16 | tf_op jit(solution)/shard_map/psum | solution.py:70
  822.9 29.9 %reduce-scatter.2.cloned.1.call-done = bf16[512,3072]{1,0:T(8,128)(2,1)} async-done(((bf16[512,6144]{1,0:T(8,128)(2,1)}), bf16[512,3072]{1,0:T(8,128)(2,1)}) %reduce-scatter.2.cloned.1.call-update) | async-done | bytes 3145744 | tf_op jit(solution)/shard_map/reduce_scatter | solution.py:67
  (66 shorter events, 7.6 us)
Async XLA Ops:
  7.2 592.8 %all-gather.3.cloned.1.call-start = ((), (), s32[]{:S(2)}) async-start(), calls=%async_computation.1 | async-start | bytes 9437184 | tf_op jit(solution)/shard_map/all_gather | solution.py:42
  7.9 748.1 %all-gather.5.cloned.1.call-start = ((), (), s32[]{:S(2)}) async-start(), calls=%async_computation.2 | async-start | bytes 20054016 | tf_op jit(solution)/shard_map/all_gather | solution.py:63
  12.5 44.9 %collective-permute-start = (bf16[384,12,384]{0,2,1:T(8,128)(2,1)S(1)}, bf16[384,12,384]{0,2,1:T(8,128)(2,1)}, u32[]{:S(2)}, u32[]{:S(2)}) collective-permute-start(bf16[384,12,384]{0,2,1:T(8,128)(2,1)S(1)} %copy.10), channel_id=1, source_target_pairs={{0,2},{2,4},{4,6},{6,8},{8,10},{10,12},{12,14},{14,16},{16,18},{18... | collective-permute-start | bytes 10616840 | tf_op jit(solution)/shard_map/ppermute | solution.py:22
  13.0 79.0 %collective-permute-start.1 = (bf16[384,12,384]{0,2,1:T(8,128)(2,1)S(1)}, bf16[384,12,384]{0,2,1:T(8,128)(2,1)}, u32[]{:S(2)}, u32[]{:S(2)}) collective-permute-start(bf16[384,12,384]{0,2,1:T(8,128)(2,1)S(1)} %copy.10), channel_id=1, source_target_pairs={{0,30},{2,0},{4,2},{6,4},{8,6},{10,8},{12,10},{14,12},{16,14},{18,... | collective-permute-start | bytes 10616840 | tf_op jit(solution)/shard_map/ppermute | solution.py:27
  57.4 44.0 %collective-permute-start.2 = (bf16[384,12,384]{0,2,1:T(8,128)(2,1)}, bf16[384,12,384]{0,2,1:T(8,128)(2,1)}, u32[]{:S(2)}, u32[]{:S(2)}) collective-permute-start(bf16[384,12,384]{0,2,1:T(8,128)(2,1)} %collective-permute-done), channel_id=1, source_target_pairs={{0,2},{2,4},{4,6},{6,8},{8,10},{10,12},{12,14},{14,16},{16,18},{18... | collective-permute-start | bytes 10616840 | tf_op jit(solution)/shard_map/ppermute | solution.py:22
  92.0 760.8 %reduce-scatter.2.cloned.1.call-start = ((), (), s32[]{:S(2)}) async-start(), calls=%async_computation.3 | async-start | bytes 9437184 | tf_op jit(solution)/shard_map/reduce_scatter | solution.py:67
  92.1 192.0 %collective-permute-start.3 = (bf16[384,12,384]{0,2,1:T(8,128)(2,1)}, bf16[384,12,384]{0,2,1:T(8,128)(2,1)S(1)}, u32[]{:S(2)}, u32[]{:S(2)}) collective-permute-start(bf16[384,12,384]{0,2,1:T(8,128)(2,1)} %collective-permute-done.1), channel_id=1, source_target_pairs={{0,30},{2,0},{4,2},{6,4},{8,6},{10,8},{12,10},{14,12},{16,14},{18,... | collective-permute-start | bytes 10616840 | tf_op jit(solution)/shard_map/ppermute | solution.py:27
  101.4 189.1 %collective-permute-start.4 = (bf16[384,12,384]{0,2,1:T(8,128)(2,1)}, bf16[384,12,384]{0,2,1:T(8,128)(2,1)S(1)}, u32[]{:S(2)}, u32[]{:S(2)}) collective-permute-start(bf16[384,12,384]{0,2,1:T(8,128)(2,1)} %collective-permute-done.2), channel_id=1, source_target_pairs={{0,2},{2,4},{4,6},{6,8},{8,10},{10,12},{12,14},{14,16},{16,18},{18... | collective-permute-start | bytes 10616840 | tf_op jit(solution)/shard_map/ppermute | solution.py:22
  284.1 1.7 copy-start.3
  285.8 86.9 %collective-permute-start.5 = (bf16[384,12,384]{0,2,1:T(8,128)(2,1)S(1)}, bf16[384,12,384]{0,2,1:T(8,128)(2,1)S(1)}, u32[]{:S(2)}, u32[]{:S(2)}) collective-permute-start(bf16[384,12,384]{0,2,1:T(8,128)(2,1)S(1)} %collective-permute-done.3), channel_id=1, source_target_pairs={{0,30},{2,0},{4,2},{6,4},{8,6},{10,8},{12,10},{14,12},{16,14},{18,... | collective-permute-start | bytes 10616840 | tf_op jit(solution)/shard_map/ppermute | solution.py:27
  290.6 82.2 %copy-start.5 = (bf16[384,12,384]{0,2,1:T(8,128)(2,1)}, bf16[384,12,384]{0,2,1:T(8,128)(2,1)S(1)}, u32[]{:S(2)}) copy-start(bf16[384,12,384]{0,2,1:T(8,128)(2,1)S(1)} %collective-permute-done.4) | copy-start | bytes 10616836
  290.6 88.0 %collective-permute-start.6 = (bf16[384,12,384]{0,2,1:T(8,128)(2,1)S(1)}, bf16[384,12,384]{0,2,1:T(8,128)(2,1)S(1)}, u32[]{:S(2)}, u32[]{:S(2)}) collective-permute-start(bf16[384,12,384]{0,2,1:T(8,128)(2,1)S(1)} %collective-permute-done.4), channel_id=1, source_target_pairs={{0,2},{2,4},{4,6},{6,8},{8,10},{10,12},{12,14},{14,16},{16,18},{18... | collective-permute-start | bytes 10616840 | tf_op jit(solution)/shard_map/ppermute | solution.py:22
  372.8 5.8 copy-start.7
  372.8 78.7 %collective-permute-start.7 = (bf16[384,12,384]{0,2,1:T(8,128)(2,1)S(1)}, bf16[384,12,384]{0,2,1:T(8,128)(2,1)S(1)}, u32[]{:S(2)}, u32[]{:S(2)}) collective-permute-start(bf16[384,12,384]{0,2,1:T(8,128)(2,1)S(1)} %collective-permute-done.5), channel_id=1, source_target_pairs={{0,30},{2,0},{4,2},{6,4},{8,6},{10,8},{12,10},{14,12},{16,14},{18,... | collective-permute-start | bytes 10616840 | tf_op jit(solution)/shard_map/ppermute | solution.py:27
  378.6 72.9 %copy-start.9 = (bf16[384,12,384]{0,2,1:T(8,128)(2,1)}, bf16[384,12,384]{0,2,1:T(8,128)(2,1)S(1)}, u32[]{:S(2)}) copy-start(bf16[384,12,384]{0,2,1:T(8,128)(2,1)S(1)} %collective-permute-done.6) | copy-start | bytes 10616836
  378.6 78.7 %collective-permute-start.8 = (bf16[384,12,384]{0,2,1:T(8,128)(2,1)S(1)}, bf16[384,12,384]{0,2,1:T(8,128)(2,1)S(1)}, u32[]{:S(2)}, u32[]{:S(2)}) collective-permute-start(bf16[384,12,384]{0,2,1:T(8,128)(2,1)S(1)} %collective-permute-done.6), channel_id=1, source_target_pairs={{0,2},{2,4},{4,6},{6,8},{8,10},{10,12},{12,14},{14,16},{16,18},{18... | collective-permute-start | bytes 10616840 | tf_op jit(solution)/shard_map/ppermute | solution.py:22
  451.5 5.8 copy-start.11
  451.5 78.8 %collective-permute-start.9 = (bf16[384,12,384]{0,2,1:T(8,128)(2,1)S(1)}, bf16[384,12,384]{0,2,1:T(8,128)(2,1)}, u32[]{:S(2)}, u32[]{:S(2)}) collective-permute-start(bf16[384,12,384]{0,2,1:T(8,128)(2,1)S(1)} %collective-permute-done.7), channel_id=1, source_target_pairs={{0,30},{2,0},{4,2},{6,4},{8,6},{10,8},{12,10},{14,12},{16,14},{18,... | collective-permute-start | bytes 10616840 | tf_op jit(solution)/shard_map/ppermute | solution.py:27
  457.3 73.0 %copy-start.13 = (bf16[384,12,384]{0,2,1:T(8,128)(2,1)}, bf16[384,12,384]{0,2,1:T(8,128)(2,1)S(1)}, u32[]{:S(2)}) copy-start(bf16[384,12,384]{0,2,1:T(8,128)(2,1)S(1)} %collective-permute-done.8) | copy-start | bytes 10616836
  457.3 79.0 %collective-permute-start.10 = (bf16[384,12,384]{0,2,1:T(8,128)(2,1)S(1)}, bf16[384,12,384]{0,2,1:T(8,128)(2,1)}, u32[]{:S(2)}, u32[]{:S(2)}) collective-permute-start(bf16[384,12,384]{0,2,1:T(8,128)(2,1)S(1)} %collective-permute-done.8), channel_id=1, source_target_pairs={{0,2},{2,4},{4,6},{6,8},{8,10},{10,12},{12,14},{14,16},{16,18},{18... | collective-permute-start | bytes 10616840 | tf_op jit(solution)/shard_map/ppermute | solution.py:22
  530.3 76.0 %collective-permute-start.11 = (bf16[384,12,384]{0,2,1:T(8,128)(2,1)}, bf16[384,12,384]{0,2,1:T(8,128)(2,1)}, u32[]{:S(2)}, u32[]{:S(2)}) collective-permute-start(bf16[384,12,384]{0,2,1:T(8,128)(2,1)} %collective-permute-done.9), channel_id=1, source_target_pairs={{0,30},{2,0},{4,2},{6,4},{8,6},{10,8},{12,10},{14,12},{16,14},{18,... | collective-permute-start | bytes 10616840 | tf_op jit(solution)/shard_map/ppermute | solution.py:27
  536.3 78.1 %collective-permute-start.12 = (bf16[384,12,384]{0,2,1:T(8,128)(2,1)}, bf16[384,12,384]{0,2,1:T(8,128)(2,1)}, u32[]{:S(2)}, u32[]{:S(2)}) collective-permute-start(bf16[384,12,384]{0,2,1:T(8,128)(2,1)} %collective-permute-done.10), channel_id=1, source_target_pairs={{0,2},{2,4},{4,6},{6,8},{8,10},{10,12},{12,14},{14,16},{16,18},{18... | collective-permute-start | bytes 10616840 | tf_op jit(solution)/shard_map/ppermute | solution.py:22
  600.0 4.6 copy-start
  600.0 50.5 %copy-start.15 = (f32[6144]{0:T(1024)S(1)}, f32[6144]{0:T(1024)}, u32[]{:S(2)}) copy-start(f32[6144]{0:T(1024)} %param.7) | copy-start | bytes 73732
  606.4 85.8 %collective-permute-start.13 = (bf16[384,12,384]{0,2,1:T(8,128)(2,1)}, bf16[384,12,384]{0,2,1:T(8,128)(2,1)S(1)}, u32[]{:S(2)}, u32[]{:S(2)}) collective-permute-start(bf16[384,12,384]{0,2,1:T(8,128)(2,1)} %collective-permute-done.11), channel_id=1, source_target_pairs={{0,30},{2,0},{4,2},{6,4},{8,6},{10,8},{12,10},{14,12},{16,14},{18,... | collective-permute-start | bytes 10616840 | tf_op jit(solution)/shard_map/ppermute | solution.py:27
  614.4 80.2 %collective-permute-start.14 = (bf16[384,12,384]{0,2,1:T(8,128)(2,1)}, bf16[384,12,384]{0,2,1:T(8,128)(2,1)S(1)}, u32[]{:S(2)}, u32[]{:S(2)}) collective-permute-start(bf16[384,12,384]{0,2,1:T(8,128)(2,1)} %collective-permute-done.12), channel_id=1, source_target_pairs={{0,2},{2,4},{4,6},{6,8},{8,10},{10,12},{12,14},{14,16},{16,18},{18... | collective-permute-start | bytes 10616840 | tf_op jit(solution)/shard_map/ppermute | solution.py:22
  656.7 4.6 copy-start.4
  656.7 6.7 copy-start.6
  661.3 4.4 copy-start.8
  663.5 4.5 copy-start.10
  665.7 4.5 copy-start.12
  668.0 4.5 copy-start.14
  734.0 10.5 %copy-start.1 = (f32[2,256,12,384]{3,1,2,0:T(8,128)S(1)}, f32[2,256,12,384]{3,1,2,0:T(8,128)}, u32[]{:S(2)}) copy-start(f32[2,256,12,384]{3,1,2,0:T(8,128)} %fusion.1) | copy-start | bytes 28311556
  734.0 10.5 %copy-start.16 = (f32[128]{0:T(128)S(1)}, f32[128]{0:T(128)}, u32[]{:S(2)}) copy-start(f32[128]{0:T(128)} %param.9) | copy-start | bytes 1540
  734.0 10.5 %copy-start.17 = (f32[128]{0:T(128)S(1)}, f32[128]{0:T(128)}, u32[]{:S(2)}) copy-start(f32[128]{0:T(128)} %param.8) | copy-start | bytes 1540
  771.6 2.0 copy-start.2
Sparse Core Ops, SparseCore 0:
  9.5 83.0 all-gather.2
  94.2 245.2 all-gather.4
  771.8 80.9 reduce-scatter.1
